TPU v7x, 32 devices: a whole 2x2x4 slice. The times are simulated.
32 devices in a mesh: vocab: 8 (over z, y), layer: 4 (over x, core).
Axes of the slice: x: 2, y: 2, z: 4, core: 2. Of those that a mesh axis runs over, the one named last changes fastest.
Arguments:
- residual: bfloat16 [1024, 8192], P('layer', 'vocab'), may hold values from -40 to 40
- gain: bfloat16 [1, 8192], P(None, 'vocab'), may hold values from 0.25 to 1.75
- unembed: bfloat16 [8192, 128256], P(None, ('vocab', 'layer')), may hold values from -0.22097087 to 0.22097087
Outputs:
- log_probs: float32 [1024, 128256], P('layer', 'vocab')
All inputs are finite; a program needn't handle non-finite values.
Results may differ from a plain program's by a relative error of at most 0.0003.
Values may be sent and summed in bfloat16 or wider, within the bound.
No kernel may reach another device: no remote copies, remote signals or barrier semaphores. Data moves between devices by JAX's collectives and lax.ppermute only.
A program may use at most 192 MiB of HBM per device.

v0:
```python
import jax
import jax.numpy as jnp
from jax import lax
from jax.sharding import PartitionSpec as P

D = 8192


def joined(shard, axis, combine):
    everything = jax.tree.map(lambda part: lax.all_gather(part, axis), shard)
    initial = jax.tree.map(lambda part: part[0], everything)

    def lap(k, so_far):
        return combine(so_far, jax.tree.map(lambda part: part[k], everything))

    return lax.fori_loop(1, lax.axis_size(axis), lap, initial)


def combine_pairs(earlier, later):
    highest = jnp.maximum(earlier[0], later[0])
    totals = earlier[1] * jnp.exp(earlier[0] - highest) + later[1] * jnp.exp(later[0] - highest)
    return (highest, totals)


def local(residual, gain, unembed):
    full_rows, full_gain = (
        lax.all_gather(residual, "vocab", axis=1, tiled=True),
        lax.all_gather(gain, "vocab", axis=1, tiled=True),
    )
    all_rows = lax.all_gather(full_rows, "layer", axis=0, tiled=True)
    widened = all_rows.astype(jnp.float32)
    squares = jnp.sum(widened * widened, axis=1)
    scaled = (widened * full_gain.astype(jnp.float32)).astype(jnp.bfloat16)
    products = jnp.dot(scaled, unembed, preferred_element_type=jnp.float32)
    inverse = lax.rsqrt(squares / D + 1e-05)
    logits = products * inverse[:, None]
    local_max = jnp.max(logits, axis=1)
    local_sums = jnp.sum(jnp.exp(logits - local_max[:, None]), axis=1)
    highest, totals = joined((local_max, local_sums), ("vocab", "layer"), combine_pairs)
    lse = highest + jnp.log(totals)
    log_values = logits - lse[:, None]
    return lax.all_to_all(log_values, "layer", split_axis=0, concat_axis=1, tiled=True)


def solution(mesh):
    placed = (P("layer", "vocab"), P(None, "vocab"), P(None, ("vocab", "layer")))
    return jax.shard_map(
        local, mesh=mesh, in_specs=placed, out_specs=P("layer", "vocab"), check_vma=False
    )
```

profile of v0, /device:TPU:0, one launch (start us, length us, event | category | flops | bytes accessed | tf_op | source)
XLA Modules:
  0.0 570.1 jit_solution(13721698906693469134)
XLA Ops:
  6.5 0.0 all-gather.5.cloned.1.call-start
  6.5 0.7 all-gather.5.cloned.1.call-update
  7.3 0.0 all-gather.7.cloned.1.call-start
  7.3 77.7 %all-gather.5.cloned.1.call-done = bf16[256,8192]{1,0:T(8,128)(2,1)} async-done(((bf16[256,1024]{1,0:T(8,128)(2,1)}), bf16[256,8192]{1,0:T(8,128)(2,1)}) %all-gather.5.cloned.1.call-update) | async-done | bytes 4194320 | tf_op jit(solution)/shard_map/all_gather | solution.py:27
  85.0 0.0 all-gather.7.cloned.1.call-update
  85.1 30.7 %all_gather.23 = bf16[1,8192]{1,0:T(2,128)(2,1)S(1)} all-gather(bf16[1,1024]{1,0:T(2,128)(2,1)} %param.6), channel_id=1, replica_groups=mesh['vocab'=8,'layer'=4] {'vocab'}, dimensions={1}, use_global_device_ids=true | all-gather | bytes 18432 | tf_op jit(solution)/shard_map/all_gather | solution.py:28
  115.9 75.2 %all-gather.7.cloned.1.call-done = bf16[1024,8192]{1,0:T(8,128)(2,1)} async-done(((bf16[256,8192]{1,0:T(8,128)(2,1)}), bf16[1024,8192]{1,0:T(8,128)(2,1)}) %all-gather.7.cloned.1.call-update) | async-done | bytes 16777232 | tf_op jit(solution)/shard_map/all_gather | solution.py:30
  191.1 7.2 %fusion.1 = f32[1024]{0:T(1024)S(1)} fusion(bf16[1024,8192]{1,0:T(8,128)(2,1)} %all-gather.7.cloned.1.call-done), kind=kLoop, calls=%fused_computation.6 | loop fusion | flops 25164800 | bytes 16781312 | tf_op jit(solution)/shard_map/reduce_sum | solution.py:32
  198.3 79.6 %multiply_reduce_fusion = (f32[1024]{0:T(1024)S(1)}, f32[1024,4008]{0,1:T(8,128)}) fusion(f32[1024]{0:T(1024)S(1)} %add_rsqrt_fusion, bf16[8192,4008]{0,1:T(8,128)(2,1)} %param.7, bf16[1024,8192]{1,0:T(8,128)(2,1)} %all-gather.7.cloned.1.call-done, f32[8192]{0:T(1024)S(1)} %bitcast.21), kind=kOutput, calls=%fused_computation.12 | convolution fusion | flops 67276455936 | bytes 98902016 | tf_op jit(solution)/shard_map/dot_general | solution.py:34
  277.9 8.4 %exponential_reduce_fusion = f32[1024]{0:T(1024)S(1)} fusion(f32[1024,4008]{0,1:T(8,128)} %get-tuple-element.155, f32[1024]{0:T(1024)S(1)} %get-tuple-element.154, f32[1024]{0:T(1024)S(1)} %add_rsqrt_fusion), kind=kLoop, calls=%fused_computation.10 | loop fusion | flops 12311552 | bytes 16429056 | tf_op jit(solution)/shard_map/reduce_sum | solution.py:38
  286.3 40.9 %all-gather.1 = f32[32768]{0:T(1024)S(1)} all-gather(f32[1024]{0:T(1024)S(1)} %exponential_reduce_fusion), channel_id=3, replica_groups=mesh['vocab'=8,'layer'=4] {'vocab','layer'}, dimensions={0}, use_global_device_ids=true | all-gather | bytes 135168 | tf_op jit(solution)/shard_map/all_gather | solution.py:10
  327.2 37.0 %all-gather = f32[32768]{0:T(1024)S(1)} all-gather(f32[1024]{0:T(1024)S(1)} %get-tuple-element.154), channel_id=2, replica_groups=mesh['vocab'=8,'layer'=4] {'vocab','layer'}, dimensions={0}, use_global_device_ids=true | all-gather | bytes 135168 | tf_op jit(solution)/shard_map/all_gather | solution.py:10
  364.2 1.8 while.17
  366.1 7.2 %multiply_subtract_fusion = f32[1024,4008]{0,1:T(8,128)S(1)} fusion(f32[1024,4008]{0,1:T(8,128)} %get-tuple-element.155, f32[1024]{0:T(1024)S(1)} %log_add_fusion, f32[1024]{0:T(1024)S(1)} %add_rsqrt_fusion), kind=kLoop, calls=%fused_computation.11 | loop fusion | flops 8208384 | bytes 32841728 | tf_op jit(solution)/shard_map/sub | solution.py:41
  373.3 1.8 copy.8
  375.1 182.2 %all_to_all.19 = f32[4,256,4008]{1,2,0:T(8,128)S(1)} all-to-all(f32[4,256,4008]{1,2,0:T(8,128)S(1)} %bitcast.17), channel_id=1, replica_groups=mesh['vocab'=8,'layer'=4] {'layer'}, dimensions={0} | all-to-all | bytes 32833536 | tf_op jit(solution)/shard_map/all_to_all | solution.py:42
  557.3 6.0 %copy.19 = f32[256,16032]{0,1:T(8,128)} copy(f32[256,16032]{0,1:T(8,128)S(1)} %bitcast.18) | data formatting | bytes 32833536
  (69 shorter events, 0.9 us)
Async XLA Ops:
  6.5 78.5 %all-gather.5.cloned.1.call-start = ((), (), s32[]{:S(2)}) async-start(), calls=%async_computation.1 | async-start | bytes 4718592 | tf_op jit(solution)/shard_map/all_gather | solution.py:27
  7.3 183.8 %all-gather.7.cloned.1.call-start = ((), (), s32[]{:S(2)}) async-start(), calls=%async_computation.2 | async-start | bytes 20971520 | tf_op jit(solution)/shard_map/all_gather | solution.py:30
Sparse Core Ops, SparseCore 0:
  9.5 75.4 all-gather.4
  86.6 104.4 all-gather.6
where the time goes:
time: 570 us
  blocking collectives  291 us (51%)
  waiting for transfers between devices  154 us (27%)
  matrix products  79.6 us (14%)
  other arithmetic  23.2 us (4%)
  between operations  13.5 us (2%)
  local copies, waits for them, and re-layouts  8.36 us (1%)
    all_to_all x1, blocking collectives, local(): lax.all_to_all(log_values, 'layer', split_axis=0, concat_axis=1, tiled=True)  182 us
    dot_general x1, matrix products, local(): products = jnp.dot(scaled, unembed, preferred_element_type=jnp.float32)  79.6 us
    all_gather x2, blocking collectives, joined(): everything = jax.tree.map(lambda part: lax.all_gather(part, axis), shard)  77.9 us
    all_gather x1, waiting for transfers between devices, local(): lax.all_gather(residual, 'vocab', axis=1, tiled=True)  77.7 us
    all_gather x1, waiting for transfers between devices, local(): all_rows = lax.all_gather(full_rows, 'layer', axis=0, tiled=True)  75.2 us
    all_gather x1, blocking collectives, local(): lax.all_gather(gain, 'vocab', axis=1, tiled=True)  30.7 us
  transfers between devices with their start and end apart: 2, of which 2 were waited for; matrix products, arithmetic and copies ran while one was open for 0% of the time, Pallas kernels for 0%

commit v1 on v0

--- a/solution.py
+++ b/solution.py
@@ -1,9 +1,19 @@
+import functools
 import jax
 import jax.numpy as jnp
 from jax import lax
 from jax.sharding import PartitionSpec as P
 
 D = 8192
+
+
+def bring_local_data(in_array, along_axis, ndim_at):
+    a_next = lax.all_gather(in_array, along_axis)
+    local_next = jnp.concatenate(a_next, axis=ndim_at)
+    return local_next
+
+
+_bind_works = functools.partial(bring_local_data, along_axis="vocab", ndim_at=1)
 
 
 def joined(shard, axis, combine):
@@ -24,7 +34,7 @@
 
 def local(residual, gain, unembed):
     full_rows, full_gain = (
-        lax.all_gather(residual, "vocab", axis=1, tiled=True),
+        _bind_works(residual),
         lax.all_gather(gain, "vocab", axis=1, tiled=True),
     )
     all_rows = lax.all_gather(full_rows, "layer", axis=0, tiled=True)

time: 570 us -> 582 us (1.021)
  local copies, waits for them, and re-layouts: 8.36 us -> 14.8 us
    reshape x0 -> x1, local copies, waits for them, and re-layouts: none -> 6.42 us  [bring_local_data(): local_next = jnp.concatenate(a_next, axis=ndim_at)]
where the time goes in v1:
time: 582 us; the launch traced here: 581 us
  blocking collectives  291 us (50%)
  waiting for transfers between devices  154 us (26%)
  matrix products  80.6 us (14%)
  other arithmetic  26.3 us (5%)
  local copies, waits for them, and re-layouts  14.8 us (3%)
  between operations  13.5 us (2%)
    all_to_all x1, blocking collectives, local(): lax.all_to_all(log_values, 'layer', split_axis=0, concat_axis=1, tiled=True)  182 us
    dot_general x1, matrix products, local(): products = jnp.dot(scaled, unembed, preferred_element_type=jnp.float32)  80.6 us
    all_gather x2, blocking collectives, joined(): everything = jax.tree.map(lambda part: lax.all_gather(part, axis), shard)  77.9 us
    all_gather x1, waiting for transfers between devices, bring_local_data(): a_next = lax.all_gather(in_array, along_axis)  77.7 us
    all_gather x1, waiting for transfers between devices, local(): all_rows = lax.all_gather(full_rows, 'layer', axis=0, tiled=True)  76 us
    all_gather x1, blocking collectives, local(): lax.all_gather(gain, 'vocab', axis=1, tiled=True)  30.7 us
  transfers between devices with their start and end apart: 2, of which 2 were waited for; matrix products, arithmetic and copies ran while one was open for 0% of the time, Pallas kernels for 0%

profile of v1, /device:TPU:0, one launch (start us, length us, event | category | flops | bytes accessed | tf_op | source)
XLA Modules:
  0.0 581.5 jit_solution(4150895280909002197)
XLA Ops:
  6.5 0.0 all-gather.8.cloned.1.call-start
  6.5 0.7 all-gather.8.cloned.1.call-update
  7.3 0.0 all-gather.6.cloned.1.call-start
  7.3 77.7 %all-gather.8.cloned.1.call-done = bf16[2048,1024]{1,0:T(8,128)(2,1)} async-done(((bf16[256,1024]{1,0:T(8,128)(2,1)}), bf16[2048,1024]{1,0:T(8,128)(2,1)}) %all-gather.8.cloned.1.call-update) | async-done | bytes 4194320 | tf_op jit(solution)/shard_map/all_gather | solution.py:11
  85.0 6.4 %copy.8 = bf16[256,8,1024]{0,2,1:T(8,128)(2,1)} copy(bf16[256,8,1024]{2,0,1:T(8,128)(2,1)} %bitcast.24) | data formatting | bytes 8388608 | tf_op jit(solution)/shard_map/reshape | solution.py:12
  91.4 0.0 all-gather.6.cloned.1.call-update
  91.5 30.7 %all_gather.27 = bf16[1,8192]{1,0:T(2,128)(2,1)S(1)} all-gather(bf16[1,1024]{1,0:T(2,128)(2,1)} %param.6), channel_id=1, replica_groups=mesh['vocab'=8,'layer'=4] {'vocab'}, dimensions={1}, use_global_device_ids=true | all-gather | bytes 18432 | tf_op jit(solution)/shard_map/all_gather | solution.py:38
  122.2 76.0 %all-gather.6.cloned.1.call-done = bf16[1024,8192]{0,1:T(8,128)(2,1)} async-done(((bf16[256,8192]{0,1:T(8,128)(2,1)}), bf16[1024,8192]{0,1:T(8,128)(2,1)}) %all-gather.6.cloned.1.call-update) | async-done | bytes 16777232 | tf_op jit(solution)/shard_map/all_gather | solution.py:40
  198.3 10.3 %fusion.1 = f32[1024]{0:T(1024)S(1)} fusion(bf16[1024,8192]{0,1:T(8,128)(2,1)} %all-gather.6.cloned.1.call-done), kind=kLoop, calls=%fused_computation.6 | loop fusion | flops 25164800 | bytes 16781312 | tf_op jit(solution)/shard_map/reduce_sum | solution.py:42
  208.6 80.6 %multiply_reduce_fusion = (f32[1024]{0:T(1024)S(1)}, f32[1024,4008]{0,1:T(8,128)}) fusion(f32[1024]{0:T(1024)S(1)} %add_rsqrt_fusion, bf16[8192,4008]{0,1:T(8,128)(2,1)} %param.7, bf16[1024,8192]{0,1:T(8,128)(2,1)} %all-gather.6.cloned.1.call-done, f32[8192]{0:T(1024)S(1)} %bitcast.27), kind=kOutput, calls=%fused_computation.12 | convolution fusion | flops 67276455936 | bytes 98902016 | tf_op jit(solution)/shard_map/dot_general | solution.py:44
  289.2 8.4 %exponential_reduce_fusion = f32[1024]{0:T(1024)S(1)} fusion(f32[1024,4008]{0,1:T(8,128)} %get-tuple-element.155, f32[1024]{0:T(1024)S(1)} %get-tuple-element.154, f32[1024]{0:T(1024)S(1)} %add_rsqrt_fusion), kind=kLoop, calls=%fused_computation.10 | loop fusion | flops 12311552 | bytes 16429056 | tf_op jit(solution)/shard_map/reduce_sum | solution.py:48
  297.6 40.9 %all-gather.2 = f32[32768]{0:T(1024)S(1)} all-gather(f32[1024]{0:T(1024)S(1)} %exponential_reduce_fusion), channel_id=4, replica_groups=mesh['vocab'=8,'layer'=4] {'vocab','layer'}, dimensions={0}, use_global_device_ids=true | all-gather | bytes 135168 | tf_op jit(solution)/shard_map/all_gather | solution.py:20
  338.5 37.0 %all-gather.1 = f32[32768]{0:T(1024)S(1)} all-gather(f32[1024]{0:T(1024)S(1)} %get-tuple-element.154), channel_id=3, replica_groups=mesh['vocab'=8,'layer'=4] {'vocab','layer'}, dimensions={0}, use_global_device_ids=true | all-gather | bytes 135168 | tf_op jit(solution)/shard_map/all_gather | solution.py:20
  375.6 1.8 while.17
  377.4 7.2 %multiply_subtract_fusion = f32[1024,4008]{0,1:T(8,128)S(1)} fusion(f32[1024,4008]{0,1:T(8,128)} %get-tuple-element.155, f32[1024]{0:T(1024)S(1)} %log_add_fusion, f32[1024]{0:T(1024)S(1)} %add_rsqrt_fusion), kind=kLoop, calls=%fused_computation.11 | loop fusion | flops 8208384 | bytes 32841728 | tf_op jit(solution)/shard_map/sub | solution.py:51
  384.6 1.8 copy.12
  386.4 182.2 %all_to_all.19 = f32[4,256,4008]{1,2,0:T(8,128)S(1)} all-to-all(f32[4,256,4008]{1,2,0:T(8,128)S(1)} %bitcast.21), channel_id=1, replica_groups=mesh['vocab'=8,'layer'=4] {'layer'}, dimensions={0} | all-to-all | bytes 32833536 | tf_op jit(solution)/shard_map/all_to_all | solution.py:52
  568.6 6.0 %copy.23 = f32[256,16032]{0,1:T(8,128)} copy(f32[256,16032]{0,1:T(8,128)S(1)} %bitcast.22) | data formatting | bytes 32833536
  (69 shorter events, 0.9 us)
Async XLA Ops:
  6.5 78.5 %all-gather.8.cloned.1.call-start = ((), (), s32[]{:S(2)}) async-start(), calls=%async_computation.2 | async-start | bytes 4718592 | tf_op jit(solution)/shard_map/all_gather | solution.py:11
  7.3 191.0 %all-gather.6.cloned.1.call-start = ((), (), s32[]{:S(2)}) async-start(), calls=%async_computation.1 | async-start | bytes 20971520 | tf_op jit(solution)/shard_map/all_gather | solution.py:40
Sparse Core Ops, SparseCore 0:
  9.5 75.5 all-gather.7
  91.6 106.6 all-gather.5
